TPU v7x, 32 devices: a whole 2x2x4 slice. The times are simulated.
32 devices in a mesh: rep: 2 (over y), dp: 16 (over z, x, core).
Axes of the slice: x: 2, y: 2, z: 4, core: 2. Of those that a mesh axis runs over, the one named last changes fastest.
Arguments:
- hidden: bfloat16 [256, 2, 3584], P(('rep', 'dp')), may hold values from -96 to 96
- lm_head: bfloat16 [3584, 12288], P(None, ('rep', 'dp')), may hold values from -0.3125 to 0.3125
- reward_head: bfloat16 [3584], replicated, may hold values from -0.09375 to 0.09375
- target_ids: int32 [256, 2], P(('rep', 'dp')), may hold values from 0 to 12287
- lengths: int32 [256], P(('rep', 'dp')), may hold values from 1 to 2
- prompt_ids: int32 [256], P(('rep', 'dp')), may hold values from 0 to 15, as said below
Outputs:
- token_logprobs: float32 [256, 2], P(('rep', 'dp'))
- advantages: float32 [256], P(('rep', 'dp'))
Inputs may be any that keep to these rules, and one draw needn't show every extreme that they name: `prompt_ids`: each prompt id names exactly 16 responses.
All inputs are finite; a program needn't handle non-finite values.
Results may differ from a plain program's by a relative error of at most 0.0003.
Values may be sent and summed in bfloat16 or wider, within the bound.
No kernel may reach another device: no remote copies, remote signals or barrier semaphores. Data moves between devices by JAX's collectives and lax.ppermute only.
A program may use at most 128 MiB of HBM per device.

v0:
```python
import jax
import jax.numpy as jnp
from jax import lax
from jax.sharding import PartitionSpec as P

GROUP = 16
PROM_DEV = 1


def moments(stacked):
    means = stacked[0] / GROUP
    scales = jnp.sqrt(jnp.maximum(stacked[1] / GROUP - means * means, 1.0))
    return (means, scales)


def local(hidden, lm_head, reward_head, target_ids, lengths, prompt_ids):
    resp_dev, window, width = hidden.shape
    voc_dev = lm_head.shape[1]
    owners = lax.axis_size("dp")
    me = lax.axis_index("rep") * owners + lax.axis_index("dp")
    tok_dev = resp_dev * window
    all_ids = lax.all_gather(target_ids.reshape(tok_dev), ("rep", "dp"), axis=0, tiled=True)
    local_ids = all_ids - me * voc_dev
    columns = lax.broadcasted_iota(jnp.int32, (1, voc_dev), 1)
    piece = lax.all_gather(hidden, ("rep", "dp"), axis=0, tiled=True)
    count = piece.shape[0] * window
    flat = piece.reshape(count, width)
    logits = jnp.dot(flat, lm_head, preferred_element_type=jnp.float32)
    peak = jnp.max(logits, axis=1)
    total = jnp.sum(jnp.exp(logits - peak[:, None]), axis=1)
    picked = jnp.sum(jnp.where(columns == local_ids[:, None], logits, 0.0), axis=1)
    totals = total
    picks = picked
    first_own = me * tok_dev
    whole_top = lax.pmax(peak, ("rep", "dp"))
    scaled = totals * jnp.exp(peak - whole_top)
    whole_total, whole_pick = lax.psum((scaled, picks), ("rep", "dp"))
    top = lax.dynamic_slice_in_dim(whole_top, first_own, tok_dev)
    total = lax.dynamic_slice_in_dim(whole_total, first_own, tok_dev)
    picked = lax.dynamic_slice_in_dim(whole_pick, first_own, tok_dev)
    logprob = (picked - (top + jnp.log(total))).reshape(resp_dev, window)
    positions = lax.broadcasted_iota(jnp.int32, (resp_dev, window), 1)
    token_logprobs = jnp.where(positions < lengths[:, None], logprob, 0.0)
    last = jnp.take_along_axis(hidden, (lengths - 1)[:, None, None], axis=1)[:, 0, :]
    rewards = jnp.dot(last, reward_head, preferred_element_type=jnp.float32)
    prompts = PROM_DEV * owners
    member = (prompt_ids[:, None] == lax.broadcasted_iota(jnp.int32, (1, prompts), 1)).astype(
        jnp.float32
    )
    sums = jnp.dot(rewards, member, precision=lax.Precision.HIGHEST)
    squares = jnp.dot(rewards * rewards, member, precision=lax.Precision.HIGHEST)
    stacked = jnp.stack([sums, squares])
    whole = lax.psum(stacked, ("rep", "dp"))
    means, scales = moments(whole)
    centre = jnp.dot(member, means, precision=lax.Precision.HIGHEST)
    spread = jnp.dot(member, scales, precision=lax.Precision.HIGHEST)
    advantages = (rewards - centre) / spread
    return (token_logprobs, advantages)


def solution(mesh):
    in_specs = (
        P(("rep", "dp"), None, None),
        P(None, ("rep", "dp")),
        P(),
        P(("rep", "dp"), None),
        P(("rep", "dp")),
        P(("rep", "dp")),
    )
    out_specs = (P(("rep", "dp"), None), P(("rep", "dp")))
    return jax.shard_map(local, mesh=mesh, in_specs=in_specs, out_specs=out_specs, check_vma=False)
```

profile of v0, /device:TPU:0, one launch (start us, length us, event | category | flops | bytes accessed | tf_op | source)
XLA Modules:
  0.0 176.3 jit_solution(201014197052093637)
XLA Ops:
  7.2 0.0 copy-start
  7.2 0.0 all-gather.2.cloned.1.call-start
  7.2 0.7 all-gather.2.cloned.1.call-update
  7.9 0.8 copy.12
  8.8 0.1 reshape.52
  8.8 0.7 reshape.54
  9.5 0.7 fusion.27
  10.2 1.6 gather_fusion
  11.8 0.2 dynamic-update-slice
  12.0 42.1 %all-reduce = s32[512]{0:T(512)S(1)} all-reduce(s32[512]{0:T(512)S(1)} %dynamic-update-slice), channel_id=1, replica_groups=mesh['rep'=2,'dp'=16] {'rep','dp'}, use_global_device_ids=true, to_apply=%add | all-reduce | flops 512 | bytes 4096
  54.1 0.7 compare_and_fusion
  54.8 0.2 fusion.2
  55.0 0.0 copy-start.1
  55.0 0.9 fusion.6
  55.8 0.9 fusion.7
  56.7 0.6 pad_maximum_fusion
  57.3 0.0 copy-done.1
  57.3 17.1 %all-gather.2.cloned.1.call-done = bf16[256,2,3584]{2,1,0:T(2,128)(2,1)} async-done(((bf16[8,2,3584]{2,1,0:T(2,128)(2,1)}), bf16[256,2,3584]{2,1,0:T(2,128)(2,1)}) %all-gather.2.cloned.1.call-update) | async-done | bytes 3670032 | tf_op jit(solution)/shard_map/all_gather | solution.py:25
  74.4 8.4 %reshape.41 = bf16[512,3584]{1,0:T(8,128)(2,1)} reshape(bf16[256,2,3584]{2,1,0:T(2,128)(2,1)} %all-gather.2.cloned.1.call-done) | data formatting | bytes 7340032 | tf_op jit(solution)/shard_map/reshape | solution.py:27
  82.8 0.0 copy-done
  82.8 3.7 %fusion.28 = (f32[512]{0:T(512)S(1)}, f32[512,384]{0,1:T(8,128)S(1)}) fusion(bf16[512,3584]{1,0:T(8,128)(2,1)} %reshape.41, bf16[3584,384]{1,0:T(8,128)(2,1)S(1)} %copy-done), kind=kOutput, calls=%fused_computation.46 | convolution fusion | flops 1409482240 | bytes 7211008 | tf_op jit(solution)/shard_map/dot_general | solution.py:28
  86.4 38.2 %pmax.7 = f32[512]{0:T(512)S(1)} all-reduce(f32[512]{0:T(512)S(1)} %get-tuple-element.13), channel_id=1, replica_groups=mesh['rep'=2,'dp'=16] {'rep','dp'}, use_global_device_ids=true, to_apply=%region_3.4 | all-reduce | flops 512 | bytes 4096 | tf_op jit(solution)/shard_map/pmax | solution.py:35
  124.7 0.2 select_reduce_fusion
  124.9 40.7 %all-reduce.1 = (f32[512]{0:T(512)S(1)}, f32[512]{0:T(512)S(1)}, f32[2,16]{1,0:T(2,128)S(1)}) all-reduce(f32[512]{0:T(512)S(1)} %exponential_multiply_fusion, f32[512]{0:T(512)S(1)} %get-tuple-element.8, f32[2,16]{1,0:T(2,128)} %pad_maximum_fusion), channel_id=1, replica_groups=mesh['rep'=2,'dp'=16] {'rep','dp'}, use_global_device_ids=true, to_apply=%region_5.6 | all-reduce | flops 1056 | bytes 8448 | tf_op jit(solution)/shard_map/psum | solution.py:37
  165.7 0.1 add_subtract_fusion
  165.8 0.1 reshape.42
  165.8 0.7 fusion.8
  166.6 0.6 copy.13
  167.2 0.8 convolution_bitcast_fusion
  168.0 1.4 fusion.1
  (6 shorter events, 0.0 us)
Async XLA Ops:
  7.2 75.6 %copy-start = (bf16[3584,384]{1,0:T(8,128)(2,1)S(1)}, bf16[3584,384]{1,0:T(8,128)(2,1)}, u32[]{:S(2)}) copy-start(bf16[3584,384]{1,0:T(8,128)(2,1)} %param.7) | copy-start | bytes 8257540
  7.2 67.2 %all-gather.2.cloned.1.call-start = ((), (), s32[]{:S(2)}) async-start(), calls=%async_computation | async-start | bytes 3784704 | tf_op jit(solution)/shard_map/all_gather | solution.py:25
  55.0 2.3 %copy-start.1 = (f32[1,8]{1,0:T(1,128)}, f32[1,8]{1,0:T(1,128)S(1)}, u32[]{:S(2)}) copy-start(f32[1,8]{1,0:T(1,128)S(1)} %fusion.2) | copy-start | bytes 100
Sparse Core Ops, SparseCore 0:
  10.8 63.4 all-gather.1
where the time goes:
time: 177 us; the launch traced here: 176 us
  blocking collectives  121 us (68%)
  waiting for transfers between devices  17.7 us (10%)
  between operations  14.1 us (8%)
  local copies, waits for them, and re-layouts  12.6 us (7%)
  matrix products  7.85 us (4%)
  other arithmetic  2.97 us (2%)
    unnamed x1, blocking collectives  42.1 us
    psum x1, blocking collectives, local(): whole_total, whole_pick = lax.psum((scaled, picks), ('rep', 'dp'))  40.7 us
    pmax x1, blocking collectives, local(): whole_top = lax.pmax(peak, ('rep', 'dp'))  38.2 us
    all_gather x1, waiting for transfers between devices, local(): piece = lax.all_gather(hidden, ('rep', 'dp'), axis=0, tiled=True)  17.1 us
    reshape x1, local copies, waits for them, and re-layouts, local(): flat = piece.reshape(count, width)  8.4 us
    dot_general x1, matrix products, local(): logits = jnp.dot(flat, lm_head, preferred_element_type=jnp.float32)  3.68 us
  transfers between devices with their start and end apart: 1, of which 1 were waited for; matrix products, arithmetic and copies ran while one was open for 4% of the time, Pallas kernels for 0%

commit v1 on v0

--- a/solution.py
+++ b/solution.py
@@ -34,7 +34,7 @@
     first_own = me * tok_dev
     whole_top = lax.pmax(peak, ("rep", "dp"))
     scaled = totals * jnp.exp(peak - whole_top)
-    whole_total, whole_pick = lax.psum((scaled, picks), ("rep", "dp"))
+    whole_total, whole_pick = lax.psum(lax.psum((scaled, picks), "dp"), "rep")
     top = lax.dynamic_slice_in_dim(whole_top, first_own, tok_dev)
     total = lax.dynamic_slice_in_dim(whole_total, first_own, tok_dev)
     picked = lax.dynamic_slice_in_dim(whole_pick, first_own, tok_dev)

time: 177 us -> 197 us (1.11)
  blocking collectives: 121 us -> 158 us
  waiting for transfers between devices: 17.7 us -> 0.68 us
    psum x1 -> x3, blocking collectives: 40.7 us -> 78.2 us  [the longest x1 42.1 us: local(): whole = lax.psum(stacked, ('rep', 'dp'))]
    all_gather x1, waiting for transfers between devices: 17.1 us -> 0.01 us  [local(): piece = lax.all_gather(hidden, ('rep', 'dp'), axis=0, tiled=True)]
    unnamed x1, blocking collectives: 42.1 us -> 40.1 us
  transfers between devices with their start and end apart: 1 -> 1, of which waited for: 1 -> 0; matrix products, arithmetic and copies ran while one was open for 4% -> 5% of each run, Pallas kernels for 0% -> 0%
where the time goes in v1:
time: 197 us; the launch traced here: 196 us
  blocking collectives  158 us (80%)
  between operations  14.1 us (7%)
  local copies, waits for them, and re-layouts  12.5 us (6%)
  matrix products  7.79 us (4%)
  other arithmetic  2.41 us (1%)
    psum x1, blocking collectives, local(): whole = lax.psum(stacked, ('rep', 'dp'))  42.1 us
    unnamed x1, blocking collectives  40.1 us
    pmax x1, blocking collectives, local(): whole_top = lax.pmax(peak, ('rep', 'dp'))  40 us
    psum x2, blocking collectives, local(): whole_total, whole_pick = lax.psum(lax.psum((scaled, picks), 'dp'), 'rep')  36 us
    reshape x1, local copies, waits for them, and re-layouts, local(): flat = piece.reshape(count, width)  8.4 us
  transfers between devices with their start and end apart: 1, of which 0 were waited for; matrix products, arithmetic and copies ran while one was open for 5% of the time, Pallas kernels for 0%

profile of v1, /device:TPU:0, one launch (start us, length us, event | category | flops | bytes accessed | tf_op | source)
XLA Modules:
  0.0 195.8 jit_solution(4325485700644569284)
XLA Ops:
  7.2 0.0 copy-start
  7.2 0.0 all-gather.2.cloned.1.call-start
  7.2 0.7 all-gather.2.cloned.1.call-update
  7.9 0.8 reshape.54
  8.7 0.7 fusion.27
  9.4 1.6 gather_fusion
  11.0 0.7 compare_and_fusion
  11.6 0.2 fusion.2
  11.8 0.9 fusion.6
  12.7 0.8 fusion.7
  13.5 42.1 %psum.39 = f32[2,16]{1,0:T(2,128)S(1)} all-reduce(f32[2,16]{1,0:T(2,128)S(1)} %pad_maximum_fusion), channel_id=1, replica_groups=mesh['rep'=2,'dp'=16] {'rep','dp'}, use_global_device_ids=true, to_apply=%region_8.9 | all-reduce | flops 32 | bytes 256 | tf_op jit(solution)/shard_map/psum | solution.py:53
  55.7 0.8 copy.12
  56.4 0.1 reshape.52
  56.5 0.2 dynamic-update-slice
  56.7 40.1 %all-reduce = s32[512]{0:T(512)S(1)} all-reduce(s32[512]{0:T(512)S(1)} %dynamic-update-slice), channel_id=1, replica_groups=mesh['rep'=2,'dp'=16] {'rep','dp'}, use_global_device_ids=true, to_apply=%add | all-reduce | flops 512 | bytes 4096
  96.8 0.8 convolution_bitcast_fusion
  97.6 1.4 fusion.1
  99.0 0.0 all-gather.2.cloned.1.call-done
  99.0 8.4 %reshape.41 = bf16[512,3584]{1,0:T(8,128)(2,1)} reshape(bf16[256,2,3584]{2,1,0:T(2,128)(2,1)} %all-gather.2.cloned.1.call-done) | data formatting | bytes 7340032 | tf_op jit(solution)/shard_map/reshape | solution.py:27
  107.4 0.0 copy-done
  107.4 3.7 %fusion.28 = (f32[512]{0:T(512)S(1)}, f32[512,384]{0,1:T(8,128)S(1)}) fusion(bf16[512,3584]{1,0:T(8,128)(2,1)} %reshape.41, bf16[3584,384]{1,0:T(8,128)(2,1)S(1)} %copy-done), kind=kOutput, calls=%fused_computation.46 | convolution fusion | flops 1409482240 | bytes 7211008 | tf_op jit(solution)/shard_map/dot_general | solution.py:28
  111.1 40.0 %pmax.7 = f32[512]{0:T(512)S(1)} all-reduce(f32[512]{0:T(512)S(1)} %get-tuple-element.14), channel_id=1, replica_groups=mesh['rep'=2,'dp'=16] {'rep','dp'}, use_global_device_ids=true, to_apply=%region_4.5 | all-reduce | flops 512 | bytes 4096 | tf_op jit(solution)/shard_map/pmax | solution.py:35
  151.1 0.2 select_reduce_fusion
  151.4 31.1 %all-reduce.1 = (f32[512]{0:T(512)S(1)}, f32[512]{0:T(512)S(1)}) all-reduce(f32[512]{0:T(512)S(1)} %exponential_multiply_fusion, f32[512]{0:T(512)S(1)} %get-tuple-element.8), channel_id=1, replica_groups=mesh['rep'=2,'dp'=16] {'dp'}, use_global_device_ids=true, to_apply=%region_6.7 | all-reduce | flops 1024 | bytes 8192 | tf_op jit(solution)/shard_map/psum | solution.py:37
  182.5 4.9 %all-reduce.2 = (f32[512]{0:T(512)S(1)}, f32[512]{0:T(512)S(1)}) all-reduce(f32[512]{0:T(512)S(1)} %get-tuple-element.10, f32[512]{0:T(512)S(1)} %get-tuple-element.11), channel_id=1, replica_groups=mesh['rep'=2,'dp'=16] {'rep'}, use_global_device_ids=true, to_apply=%region_7.8 | all-reduce | flops 1024 | bytes 8192 | tf_op jit(solution)/shard_map/psum | solution.py:37
  187.4 0.1 add_subtract_fusion
  187.5 0.1 reshape.42
  187.6 0.7 fusion.8
  188.3 0.6 copy.13
  (7 shorter events, 0.0 us)
Async XLA Ops:
  7.2 100.2 %copy-start = (bf16[3584,384]{1,0:T(8,128)(2,1)S(1)}, bf16[3584,384]{1,0:T(8,128)(2,1)}, u32[]{:S(2)}) copy-start(bf16[3584,384]{1,0:T(8,128)(2,1)} %param.7) | copy-start | bytes 8257540
  7.2 91.8 %all-gather.2.cloned.1.call-start = ((), (), s32[]{:S(2)}) async-start(), calls=%async_computation | async-start | bytes 3784704 | tf_op jit(solution)/shard_map/all_gather | solution.py:25
Sparse Core Ops, SparseCore 0:
  10.8 63.0 all-gather.1
